TPU v7x, 128 devices: a whole 4x4x4 slice. The times are simulated.
128 devices in a mesh: dp: 4 (over x), expert: 32 (over y, z, core).
Axes of the slice: x: 4, y: 4, z: 4, core: 2. Of those that a mesh axis runs over, the one named last changes fastest.
Arguments:
- hidden: bfloat16 [196608, 1024], P(('dp', 'expert')), may hold values from -24 to 24
- dout: bfloat16 [196608, 7168], P(('dp', 'expert')), may hold values from -1536 to 1536
- counts: int32 [128, 256], P(('dp', 'expert')), may hold values from 1 to 1536, as said below
- bucket_expert: int32 [1], replicated, may hold values from 0 to 255
- param: float32 [1024, 7168], P(('dp', 'expert')), may hold values from -0.1875 to 0.1875
- momentum: float32 [1024, 7168], P(('dp', 'expert')), may hold values from -3 to 3
Outputs:
- new_param: float32 [1024, 7168], P(('dp', 'expert'))
- new_momentum: float32 [1024, 7168], P(('dp', 'expert'))
- direction: float32 [1024, 7168], P(('dp', 'expert'))
Inputs may be any that keep to these rules, and one draw needn't show every extreme that they name: `counts`: row k is device k's count; its rows k * 1536 + t with t below the count are live. For every expert some device has exactly 1536.
All inputs are finite; a program needn't handle non-finite values.
Results may differ from a plain program's by a relative error of at most 0.0003.
Values sent between devices are 32-bit elements; how exact they have to be, the bound alone decides.
A program may use at most 128 MiB of HBM per device.

v0:
```python
import jax
import jax.numpy as jnp
from jax import lax
from jax.sharding import Mesh
from jax.sharding import PartitionSpec as P

DP_EXPERT = ("dp", "expert_0", "expert_1", "expert_2")
EXPERT = ("expert_0", "expert_1", "expert_2")


first_beta = 0.9
second_beta = 0.99
decay_rate = 0.1
learn_rate = 0.001
soft_width = 0.05


def one_axis_at_a_time(x, axes):
    for axis in axes:
        x = lax.psum(x, axis)
    return x


def split_up(x, dim, count):
    before, after = (x.shape[:dim], x.shape[dim + 1 :])
    return jnp.moveaxis(x.reshape(*before, count, -1, *after), dim, 0)


def sum_at_owner(x, axis, dim):
    blocks = split_up(x, dim, lax.axis_size(axis))
    arrived = lax.all_to_all(blocks, axis, split_axis=0, concat_axis=0, tiled=True)
    return arrived.sum(axis=0)


def block_product(columns, dout):
    dims = (((0,), (0,)), ((), ()))
    return lax.dot_general(columns, dout, dims, preferred_element_type=jnp.float32)


def body(hidden, dout, counts, bucket_expert, param, momentum):
    rows_local = hidden.shape[0]
    width = hidden.shape[1]
    catalog = lax.broadcasted_iota(jnp.int32, counts.shape, 1)
    own_count = jnp.sum(jnp.where(catalog == bucket_expert[0], counts, 0))
    position = lax.broadcasted_iota(jnp.int32, (rows_local, 1), 0)
    masked = jnp.where(position < own_count, hidden, jnp.zeros_like(hidden))
    total = one_axis_at_a_time(own_count, DP_EXPERT).astype(jnp.float32)
    divisor = jnp.float32(1.0)
    replicas = lax.axis_size("dp")
    owners = lax.axis_size(EXPERT)
    piece = width // (replicas * owners)
    reordered = (
        masked.reshape(rows_local, replicas, owners, piece)
        .transpose(0, 2, 1, 3)
        .reshape(rows_local, width)
    )
    share = lax.psum_scatter(
        block_product(reordered, dout) / divisor, EXPERT, scatter_dimension=0, tiled=True
    )
    shard = sum_at_owner(share, "dp", 0)
    grad = shard / total
    blend = first_beta * momentum + (1.0 - first_beta) * grad
    direction = jnp.tanh(blend / soft_width) + decay_rate * param
    new_param = param - learn_rate * direction
    new_momentum = second_beta * momentum + (1.0 - second_beta) * grad
    return (new_param, new_momentum, direction)


def solution(mesh):
    split = Mesh(
        mesh.devices.reshape(mesh.shape["dp"], 4, 4, 2), ("dp", "expert_0", "expert_1", "expert_2")
    )
    in_specs = (
        P(DP_EXPERT, None),
        P(DP_EXPERT, None),
        P(DP_EXPERT, None),
        P(),
        P(DP_EXPERT, None),
        P(DP_EXPERT, None),
    )
    out_specs = (P(DP_EXPERT, None), P(DP_EXPERT, None), P(DP_EXPERT, None))
    return jax.shard_map(body, mesh=split, in_specs=in_specs, out_specs=out_specs, check_vma=False)
```

profile of v0, /device:TPU:0, one launch (start us, length us, event | category | flops | bytes accessed | tf_op | source)
XLA Modules:
  0.0 247.7 jit_solution(3786122507346543046)
XLA Ops:
  7.2 0.0 reduce-scatter.2.cloned.1.call-start
  7.9 1.3 fusion
  9.2 0.7 iota_compare_fusion
  9.8 3.2 %copy.9 = bf16[1536,1024]{0,1:T(8,128)(2,1)S(1)} copy(bf16[1536,1024]{1,0:T(8,128)(2,1)} %param.6) | data formatting | bytes 6291456 | tf_op args[0]
  13.0 0.2 broadcast_select_fusion
  13.2 0.4 copy.10
  13.7 29.0 %fusion.1 = f32[1024,7168]{1,0:T(8,128)} fusion(bf16[1536,1024]{0,1:T(8,128)(2,1)S(1)} %bitcast.10, bf16[1536,7168]{1,0:T(8,128)(2,1)} %param.7), kind=kOutput, calls=%fused_computation.8 | convolution fusion | flops 22548578304 | bytes 54525952 | tf_op jit(solution)/shard_map/dot_general | solution.py:37
  42.6 0.0 reduce-scatter.2.cloned.1.call-update
  42.6 0.0 copy-start
  42.7 0.0 copy-start.1
  42.7 156.7 %reduce-scatter.2.cloned.1.call-done = f32[32,7168]{1,0:T(8,128)} async-done(((f32[1024,7168]{1,0:T(8,128)}), f32[32,7168]{1,0:T(8,128)}) %reduce-scatter.2.cloned.1.call-update) | async-done | bytes 917520 | tf_op jit(solution)/shard_map/reduce_scatter | solution.py:57
  199.3 4.2 %all-to-all-start = ((f32[4,8,7168]{2,1,0:T(8,128)}), f32[4,8,7168]{2,1,0:T(8,128)S(1)}, u32[]{:S(2)}, u32[]{:S(2)}) async-start(f32[4,8,7168]{2,1,0:T(8,128)} %bitcast.11), calls=%async_computation.1 | async-start | bytes 1835008 | tf_op jit(solution)/shard_map/all_to_all | solution.py:31
  203.6 16.7 %psum.28 = s32[]{:T(128)} all-reduce(s32[]{:T(128)} %fusion), channel_id=1, replica_groups=mesh['dp'=4,'expert_0'=4,'expert_1'=4,'expert_2'=2] {'dp'}, use_global_device_ids=true, to_apply=%region_3.4 | all-reduce | flops 1 | bytes 8 | tf_op jit(solution)/shard_map/psum | solution.py:20
  220.3 8.5 %psum.29 = s32[]{:T(128)} all-reduce(s32[]{:T(128)} %psum.28), channel_id=1, replica_groups=mesh['dp'=4,'expert_0'=4,'expert_1'=4,'expert_2'=2] {'expert_0'}, use_global_device_ids=true, to_apply=%region_4.5 | all-reduce | flops 1 | bytes 8 | tf_op jit(solution)/shard_map/psum | solution.py:20
  228.7 8.0 %psum.30 = s32[]{:T(128)} all-reduce(s32[]{:T(128)} %psum.29), channel_id=1, replica_groups=mesh['dp'=4,'expert_0'=4,'expert_1'=4,'expert_2'=2] {'expert_1'}, use_global_device_ids=true, to_apply=%region_5.6 | all-reduce | flops 1 | bytes 8 | tf_op jit(solution)/shard_map/psum | solution.py:20
  236.8 2.4 psum.31
  239.9 0.0 all-to-all-done
  239.9 0.1 reduce_sum.19
  239.9 0.0 copy-done
  239.9 0.0 copy-done.1
  239.9 0.9 multiply_subtract_fusion
Async XLA Ops:
  7.2 192.2 %reduce-scatter.2.cloned.1.call-start = ((), (), s32[]{:S(2)}) async-start(), calls=%async_computation.2 | async-start | bytes 30277632 | tf_op jit(solution)/shard_map/reduce_scatter | solution.py:57
  42.6 197.3 %copy-start = (f32[8,7168]{1,0:T(8,128)S(1)}, f32[8,7168]{1,0:T(8,128)}, u32[]{:S(2)}) copy-start(f32[8,7168]{1,0:T(8,128)} %param.10) | copy-start | bytes 688132
  42.7 197.3 %copy-start.1 = (f32[8,7168]{1,0:T(8,128)S(1)}, f32[8,7168]{1,0:T(8,128)}, u32[]{:S(2)}) copy-start(f32[8,7168]{1,0:T(8,128)} %param.11) | copy-start | bytes 688132
  199.3 40.5 %all-to-all-start = ((f32[4,8,7168]{2,1,0:T(8,128)}), f32[4,8,7168]{2,1,0:T(8,128)S(1)}, u32[]{:S(2)}, u32[]{:S(2)}) async-start(f32[4,8,7168]{2,1,0:T(8,128)} %bitcast.11), calls=%async_computation.1 | async-start | bytes 1835008 | tf_op jit(solution)/shard_map/all_to_all | solution.py:31
Sparse Core Ops, SparseCore 0:
  42.8 156.5 reduce-scatter.1
where the time goes:
time: 249 us; the launch traced here: 248 us
  waiting for transfers between devices  157 us (63%)
  blocking collectives  35.6 us (14%)
  matrix products  29 us (12%)
  between operations  15.4 us (6%)
  starting transfers between devices  4.27 us (2%)
  local copies, waits for them, and re-layouts  3.6 us (1%)
  other arithmetic  3.17 us (1%)
    reduce_scatter x1, waiting for transfers between devices, body(): lax.psum_scatter(block_product(reordered, dout) / divisor, EXPERT, scatte...  157 us
    psum x4, blocking collectives, one_axis_at_a_time(): x = lax.psum(x, axis)  35.6 us
    dot_general x1, matrix products, block_product(): lax.dot_general(columns, dout, dims, preferred_element_type=jnp.float32)  29 us
  transfers between devices with their start and end apart: 2, of which 1 were waited for; matrix products, arithmetic and copies ran while one was open for 0% of the time, Pallas kernels for 0%

commit v1 on v0

v1 whole, which is shorter than its diff:
```python
import jax
import jax.numpy as jnp
from jax import lax
from jax.experimental import pallas as pl
from jax.experimental.pallas import tpu as pltpu
from jax.sharding import Mesh
from jax.sharding import PartitionSpec as P

AXES = ("x", "y", "z", "c")
MESH = pl.DeviceIdType.MESH

first_beta = 0.9
second_beta = 0.99
decay_rate = 0.1
learn_rate = 0.001
soft_width = 0.05

ROWS = 1536
WIDTH = 1024
PAIR = 256
PAIRS = 28
THEIR_SLOTS = 6
DOUT_SLOTS = 4
HIDDEN_CHUNKS = 4

GROUPS = ((1, 1, 1), (2, 2, 2), (2, 2, 2), (2, 2, 2), (2, 1, 1), (1, 1, 1))
ORDERS = ((0, 2, 1), (1, 0, 2), (2, 1, 0))


def plan():
    groups = []
    pair = 0
    number = 0
    for sizes in GROUPS:
        units = []
        for colour, size in enumerate(sizes):
            if size:
                units.append((number, ORDERS[colour], pair, size))
                number += 1
                pair += size
        groups.append(units)
    assert pair == PAIRS
    return groups, number


PLAN, UNITS = plan()


def kernel(
    counts_ref,
    bucket_ref,
    hidden_ref,
    dout_ref,
    sum_ref,
    total_ref,
    hidden_buf,
    lhs,
    dout_buf,
    acc,
    crossed,
    first_in,
    second_in,
    third_in,
    tally,
    tally_in,
    hidden_sem,
    dout_sem,
    cross_send,
    cross_recv,
    first_send,
    first_hop,
    first_rest,
    second_send,
    second_hop,
    second_rest,
    third_send,
    third_recv,
    tally_send,
    tally_recv,
):
    me = tuple(lax.axis_index(axis) for axis in AXES)
    core = me[3]

    def shifted(dim, by):
        return lax.rem(me[dim] + by, 4)

    def peer(dim, by):
        return tuple(shifted(dim, by) if axis == dim else me[axis] for axis in range(4))

    partner = (me[0], me[1], me[2], 1 - core)

    barrier = pltpu.get_barrier_semaphore()
    pl.semaphore_signal(barrier, inc=1, device_id=partner, device_id_type=MESH)
    for dim in range(3):
        for by in (1, 2, 3):
            pl.semaphore_signal(barrier, inc=1, device_id=peer(dim, by), device_id_type=MESH)

    chunk = ROWS // HIDDEN_CHUNKS

    def hidden_copy(part):
        rows = pl.ds(part * chunk, chunk)
        return pltpu.make_async_copy(hidden_ref.at[rows], hidden_buf.at[rows], hidden_sem.at[part])

    def dout_copy(pair):
        slot = lax.rem(pair, DOUT_SLOTS)
        columns = pl.ds(pl.multiple_of(pair * PAIR, PAIR), PAIR)
        return pltpu.make_async_copy(dout_ref.at[:, columns], dout_buf.at[slot], dout_sem.at[slot])

    for part in range(HIDDEN_CHUNKS):
        hidden_copy(part).start()
    for pair in range(DOUT_SLOTS - 1):
        dout_copy(pair).start()

    own_count = counts_ref[0, bucket_ref[0]]

    for part in range(HIDDEN_CHUNKS):
        hidden_copy(part).wait()

        def turn(step, carry, part=part):
            row = pl.multiple_of(part * chunk + step * 128, 128)
            position = lax.broadcasted_iota(jnp.int32, (128, WIDTH), 0) + row
            live = jnp.where(position < own_count, 1.0, 0.0).astype(jnp.bfloat16)
            masked = hidden_buf[pl.ds(row, 128), :] * live
            lhs[:, pl.ds(row, 128)] = masked.T
            return carry

        lax.fori_loop(0, chunk // 128, turn, 0)

    tally[0] = jnp.full((8, 128), own_count, jnp.int32).astype(jnp.float32)

    pl.semaphore_wait(barrier, 10)

    def remote(source, target, send, recv, device):
        return pltpu.make_async_remote_copy(
            src_ref=source,
            dst_ref=target,
            send_sem=send,
            recv_sem=recv,
            device_id=device,
            device_id_type=MESH,
        )

    def arrived(target, recv):
        remote(target, target, recv, recv, partner).wait_recv()

    def left(source, send):
        remote(source, source, send, send, partner).wait_send()

    def cross_copy(pair):
        slot = lax.rem(pair, THEIR_SLOTS)
        return remote(acc.at[slot], crossed.at[pair], cross_send.at[slot], cross_recv.at[pair], partner)

    def product(pair, carry):
        slot = lax.rem(pair, DOUT_SLOTS)
        dout_copy(pair).wait()

        @pl.when(pair + (DOUT_SLOTS - 1) < PAIRS)
        def _():
            dout_copy(pair + (DOUT_SLOTS - 1)).start()

        @pl.when(pair >= THEIR_SLOTS)
        def _():
            left(acc.at[lax.rem(pair, THEIR_SLOTS)], cross_send.at[lax.rem(pair, THEIR_SLOTS)])

        theirs = lax.rem(pair, THEIR_SLOTS)
        mine = THEIR_SLOTS + pair
        place_0 = core * theirs + (1 - core) * mine
        place_1 = core * mine + (1 - core) * theirs
        for half in range(2):
            rows = pl.ds(half * (WIDTH // 2), WIDTH // 2)
            value = jnp.dot(lhs[rows, :], dout_buf[slot], preferred_element_type=jnp.float32)
            value = value.reshape(2, 4, 4, 2, 8, PAIR)
            acc[place_0, 2 * half : 2 * half + 2] = value[:, :, :, 0]
            acc[place_1, 2 * half : 2 * half + 2] = value[:, :, :, 1]
        cross_copy(pair).start()
        return carry

    def products(group):
        lax.fori_loop(group[0][2], group[-1][2] + group[-1][3], product, 0)

    def at(where):
        return tuple(where.get(dim, slice(None)) for dim in range(3))

    def half_of(side):
        return pl.ds(2 * side, 2)

    def first_region(order, place, side):
        cut = min(order[1], order[2])
        return at({order[0]: place, cut: half_of(side)})

    def second_region(order, place, side):
        return at({order[0]: me[order[0]], order[1]: place, order[2]: half_of(side)})

    def third_region(order, place):
        return at({order[0]: me[order[0]], order[1]: me[order[1]], order[2]: place})

    def gather(pair, size, region, terms):
        for step in range(size):
            spot = (THEIR_SLOTS + pair + step,) + region
            value = acc[spot]
            for ref, index in terms:
                value = value + ref[(pair + step,) + index]
            acc[spot] = value

    def first_copy(unit, kind):
        number, order, pair, size = unit
        by = (2, 2, 1, 3, 1, 3)[kind]
        side = (0, 1, 1, 0, 0, 1)[kind]
        region = first_region(order, shifted(order[0], by), side)
        recv = first_hop if kind < 2 else first_rest
        copy = remote(
            acc.at[(pl.ds(THEIR_SLOTS + pair, size),) + region],
            first_in.at[pl.ds(pair, size), kind],
            first_send.at[number],
            recv.at[number],
            peer(order[0], (1, 3)[kind % 2]),
        )
        return copy, region

    def second_copy(unit, kind):
        number, order, pair, size = unit
        by = (2, 2, 1, 3, 1, 3)[kind]
        side = (0, 1, 1, 0, 0, 1)[kind]
        region = second_region(order, shifted(order[1], by), side)
        recv = second_hop if kind < 2 else second_rest
        copy = remote(
            acc.at[(pl.ds(THEIR_SLOTS + pair, size),) + region],
            second_in.at[pl.ds(pair, size), kind],
            second_send.at[number],
            recv.at[number],
            peer(order[1], (1, 3)[kind % 2]),
        )
        return copy, region

    def third_copy(unit, by):
        number, order, pair, size = unit
        return remote(
            acc.at[(pl.ds(THEIR_SLOTS + pair, size),) + third_region(order, shifted(order[2], by))],
            third_in.at[pl.ds(pair, size), by - 1],
            third_send.at[number],
            third_recv.at[number],
            peer(order[2], by),
        )

    def stage_1(unit):
        number, order, pair, size = unit
        for step in range(size):
            arrived(crossed.at[pair + step], cross_recv.at[pair + step])
        for kind in range(4):
            copy, region = first_copy(unit, kind)
            gather(pair, size, region, ((crossed, region),))
            copy.start()

    def stage_2(unit):
        number, order, pair, size = unit
        arrived(first_in.at[pl.ds(pair, size), pl.ds(0, 2)], first_hop.at[number])
        for kind in (4, 5):
            copy, region = first_copy(unit, kind)
            gather(pair, size, region, ((crossed, region), (first_in, (kind - 4,))))
            copy.start()

    def stage_3(unit):
        number, order, pair, size = unit
        arrived(first_in.at[pl.ds(pair, size), pl.ds(2, 4)], first_rest.at[number])
        left(first_in.at[pl.ds(pair, size)], first_send.at[number])
        for side, (up, down) in enumerate(((4, 3), (2, 5))):
            region = first_region(order, me[order[0]], side)
            gather(pair, size, region, ((crossed, region), (first_in, (up,)), (first_in, (down,))))
        for kind in range(4):
            second_copy(unit, kind)[0].start()

    def stage_4(unit):
        number, order, pair, size = unit
        arrived(second_in.at[pl.ds(pair, size), pl.ds(0, 2)], second_hop.at[number])
        for kind in (4, 5):
            copy, region = second_copy(unit, kind)
            gather(pair, size, region, ((second_in, (kind - 4,)),))
            copy.start()

    def stage_5(unit):
        number, order, pair, size = unit
        arrived(second_in.at[pl.ds(pair, size), pl.ds(2, 4)], second_rest.at[number])
        left(second_in.at[pl.ds(pair, size)], second_send.at[number])
        for side, (up, down) in enumerate(((4, 3), (2, 5))):
            region = second_region(order, me[order[1]], side)
            gather(pair, size, region, ((second_in, (up,)), (second_in, (down,))))
        for by in (1, 2, 3):
            third_copy(unit, by).start()

    def stage_6(unit):
        number, order, pair, size = unit
        arrived(third_in.at[pl.ds(pair, size)], third_recv.at[number])
        left(third_in.at[pl.ds(pair, size)], third_send.at[number])
        region = third_region(order, me[order[2]])
        for step in range(size):
            value = acc[(THEIR_SLOTS + pair + step,) + region]
            for by in range(3):
                value = value + third_in[pair + step, by]
            sum_ref[:, pl.ds((pair + step) * PAIR, PAIR)] = value

    def tally_start(level):
        if level == 0:
            remote(tally.at[0], tally_in.at[0, 0], tally_send.at[0], tally_recv.at[0], partner).start()
        else:
            for by in (1, 2, 3):
                remote(
                    tally.at[level],
                    tally_in.at[level, by - 1],
                    tally_send.at[level],
                    tally_recv.at[level],
                    peer(level - 1, by),
                ).start()

    def tally_end(level):
        number = 1 if level == 0 else 3
        arrived(tally_in.at[level, pl.ds(0, number)], tally_recv.at[level])
        left(tally_in.at[level, pl.ds(0, number)], tally_send.at[level])
        value = tally[level]
        for by in range(number):
            value = value + tally_in[level, by]
        tally[level + 1] = value

    stages = (stage_1, stage_2, stage_3, stage_4, stage_5, stage_6)
    tally_start(0)
    products(PLAN[0])
    for step in range(len(PLAN) + len(stages) - 1):
        if step + 1 < len(PLAN):
            products(PLAN[step + 1])
        for lag, stage in enumerate(stages):
            if 0 <= step - lag < len(PLAN):
                for unit in PLAN[step - lag]:
                    stage(unit)
        if step < 4:
            tally_end(step)
            if step < 3:
                tally_start(step + 1)
    total_ref[...] = tally[4]
    for slot in range(THEIR_SLOTS):
        left(acc.at[slot], cross_send.at[slot])


def reduced(counts, bucket_expert, hidden, dout):
    f32 = jnp.float32
    dma = pltpu.SemaphoreType.DMA
    vmem = pl.BlockSpec(memory_space=pltpu.VMEM)
    smem = pl.BlockSpec(memory_space=pltpu.SMEM)
    away = pl.BlockSpec(memory_space=pl.ANY)
    return pl.pallas_call(
        kernel,
        out_shape=(
            jax.ShapeDtypeStruct((8, PAIR * PAIRS), f32),
            jax.ShapeDtypeStruct((8, 128), f32),
        ),
        in_specs=[smem, smem, away, away],
        out_specs=(vmem, vmem),
        scratch_shapes=[
            pltpu.VMEM((ROWS, WIDTH), jnp.bfloat16),
            pltpu.VMEM((WIDTH, ROWS), jnp.bfloat16),
            pltpu.VMEM((DOUT_SLOTS, ROWS, PAIR), jnp.bfloat16),
            pltpu.VMEM((THEIR_SLOTS + PAIRS, 4, 4, 4, 8, PAIR), f32),
            pltpu.VMEM((PAIRS, 4, 4, 4, 8, PAIR), f32),
            pltpu.VMEM((PAIRS, 6, 2, 4, 8, PAIR), f32),
            pltpu.VMEM((PAIRS, 6, 2, 8, PAIR), f32),
            pltpu.VMEM((PAIRS, 3, 8, PAIR), f32),
            pltpu.VMEM((5, 8, 128), f32),
            pltpu.VMEM((4, 3, 8, 128), f32),
            dma((HIDDEN_CHUNKS,)),
            dma((DOUT_SLOTS,)),
            dma((THEIR_SLOTS,)),
            dma((PAIRS,)),
            dma((UNITS,)),
            dma((UNITS,)),
            dma((UNITS,)),
            dma((UNITS,)),
            dma((UNITS,)),
            dma((UNITS,)),
            dma((UNITS,)),
            dma((UNITS,)),
            dma((4,)),
            dma((4,)),
        ],
        compiler_params=pltpu.CompilerParams(
            collective_id=0, has_side_effects=True, vmem_limit_bytes=67043328
        ),
    )(counts, bucket_expert, hidden, dout)


def body(hidden, dout, counts, bucket_expert, param, momentum):
    summed, total = reduced(counts, bucket_expert, hidden, dout)
    grad = summed / total[0, 0]
    blend = first_beta * momentum + (1.0 - first_beta) * grad
    direction = jnp.tanh(blend / soft_width) + decay_rate * param
    new_param = param - learn_rate * direction
    new_momentum = second_beta * momentum + (1.0 - second_beta) * grad
    return (new_param, new_momentum, direction)


def solution(mesh):
    split = Mesh(mesh.devices.reshape(4, 4, 4, 2), AXES)
    rows = P(AXES, None)
    return jax.shard_map(
        body,
        mesh=split,
        in_specs=(rows, rows, rows, P(), rows, rows),
        out_specs=(rows, rows, rows),
        check_vma=False,
    )
```

time: 249 us -> 92.3 us (0.37)
  waiting for transfers between devices: 157 us -> 0 us
  Pallas kernels: 0 us -> 86.9 us
  blocking collectives: 35.6 us -> 0 us
  matrix products: 29 us -> 0 us
  between operations: 15.4 us -> 1.29 us
  starting transfers between devices: 4.27 us -> 0 us
    reduce_scatter x1 -> x0, waiting for transfers between devices: 157 us -> none  [body(): lax.psum_scatter(block_product(reordered, dout) / divisor, EXPERT, scatte...]
    pallas_call x0 -> x1, Pallas kernels: none -> 86.9 us  [reduced(): pl.pallas_call(kernel, out_shape=(jax.ShapeDtypeStruct((8, PAIR * PAIRS),...]
    psum x4 -> x0, blocking collectives: 35.6 us -> none  [one_axis_at_a_time(): x = lax.psum(x, axis)]
    dot_general x1 -> x0, matrix products: 29 us -> none  [block_product(): lax.dot_general(columns, dout, dims, preferred_element_type=jnp.float32)]
    all_to_all x1 -> x0, starting transfers between devices: 4.24 us -> none  [sum_at_owner(): lax.all_to_all(blocks, axis, split_axis=0, concat_axis=0, tiled=True)]
    unnamed x5 -> x0, local copies, waits for them, and re-layouts: 3.2 us -> none
  transfers between devices with their start and end apart: 2 -> 0, of which waited for: 1 -> 0; matrix products, arithmetic and copies ran while one was open for 0% -> 0% of each run, Pallas kernels for 0% -> 0%
where the time goes in v1:
time: 92.3 us; the launch traced here: 92.1 us
  Pallas kernels  86.9 us (94%)
  other arithmetic  2.72 us (3%)
  between operations  1.29 us (1%)
  local copies, waits for them, and re-layouts  1.21 us (1%)
    pallas_call x1, Pallas kernels, reduced(): pl.pallas_call(kernel, out_shape=(jax.ShapeDtypeStruct((8, PAIR * PAIRS),...  86.9 us
    sub x1, other arithmetic, body(): new_param = param - learn_rate * direction  2.72 us

profile of v1, /device:TPU:0, one launch (start us, length us, event | category | flops | bytes accessed | tf_op | source)
XLA Modules:
  0.0 92.1 jit_solution(9401413397942456321)
XLA Ops:
  1.3 86.9 %shard_map.85 = (f32[8,7168]{1,0:T(8,128)}, f32[8,128]{1,0:T(8,128)}) custom-call(s32[1,256]{1,0:T(1,128)} %counts_ref.1, s32[1]{0:T(128)S(6)} %copy.9.bucket_ref, bf16[1536,1024]{1,0:T(8,128)(2,1)} %hidden_ref.1, bf16[1536,7168]{1,0:T(8,128)(2,1)} %dout_ref.1), custom_call_target="tpu_custom_call" | custom-call | tf_op jit(solution)/shard_map/pallas_call | solution.py:348
  88.2 1.2 %slice.3 = f32[1,1]{1,0:T(1,128)} slice(f32[8,128]{1,0:T(8,128)} %get-tuple-element.6), slice={[0:1], [0:1]} | slice | bytes 8 | tf_op jit(solution)/shard_map/slice | solution.py:390
  89.4 2.7 %multiply_subtract_fusion = (f32[8,7168]{1,0:T(8,128)}, f32[8,7168]{1,0:T(8,128)}, f32[8,7168]{1,0:T(8,128)}) fusion(f32[8,7168]{1,0:T(8,128)} %param.10, f32[8,7168]{1,0:T(8,128)} %get-tuple-element.5, f32[]{:T(128)} %bitcast, f32[8,7168]{1,0:T(8,128)} %param.11), kind=kLoop, calls=%fused_computation.1 | loop fusion | flops 688128 | bytes 1376260 | tf_op jit(solution)/shard_map/sub | solution.py:393

commit v2 on v1

--- a/solution.py
+++ b/solution.py
@@ -21,29 +21,82 @@
 PAIRS = 28
 THEIR_SLOTS = 6
 DOUT_SLOTS = 4
-HIDDEN_CHUNKS = 4
-
-GROUPS = ((1, 1, 1), (2, 2, 2), (2, 2, 2), (2, 2, 2), (2, 1, 1), (1, 1, 1))
+HIDDEN_CHUNKS = 6
+
+SIZES = (
+    (1, 1, 1, 1, 1, 1, 1, 1, 1, 1),
+    (1, 1, 1, 1, 1, 1, 1, 1, 1),
+    (1, 1, 1, 1, 1, 1, 1, 1, 1),
+)
 ORDERS = ((0, 2, 1), (1, 0, 2), (2, 1, 0))
-
-
-def plan():
-    groups = []
+SWAPPED = ((3, 6), (2, 4, 6), ())
+LEAD = 3
+BLOCK = 4
+TALLY_AFTER = (3, 9, 15, 21)
+
+
+def make_units():
+    units = []
     pair = 0
-    number = 0
-    for sizes in GROUPS:
-        units = []
-        for colour, size in enumerate(sizes):
-            if size:
-                units.append((number, ORDERS[colour], pair, size))
-                number += 1
-                pair += size
-        groups.append(units)
+    for turn in range(max(len(sizes) for sizes in SIZES)):
+        for colour, sizes in enumerate(SIZES):
+            if turn < len(sizes):
+                order = ORDERS[colour]
+                if turn in SWAPPED[colour]:
+                    order = (order[0], order[2], order[1])
+                units.append((len(units), order, pair, sizes[turn]))
+                pair += sizes[turn]
     assert pair == PAIRS
-    return groups, number
-
-
-PLAN, UNITS = plan()
+    return units
+
+
+def list_schedule(units):
+    product_us, cross_us, latency_us, piece_us = 1.03, 0.85, 2.0, 1.405
+    free = {(dim, way): 0.0 for dim in range(3) for way in range(2)}
+    level = [0] * len(units)
+    ready = [None] * len(units)
+    rest = [0.0] * len(units)
+    crossed = []
+    cross_free = 0.0
+    now = 0.0
+    order = []
+
+    def send(dim, way, duration):
+        free[dim, way] = max(free[dim, way], now) + duration
+        return free[dim, way] + latency_us
+
+    while min(level) < 6:
+        for number, (_, _, pair, size) in enumerate(units):
+            if level[number] == 0 and pair + size <= len(crossed):
+                ready[number] = max(crossed[pair : pair + size])
+        waiting = [n for n in range(len(units)) if level[n] < 6 and ready[n] is not None]
+        first = min(waiting, key=lambda n: (ready[n], n), default=None)
+        if len(crossed) < PAIRS and (len(crossed) < LEAD or first is None or ready[first] > now):
+            now += product_us
+            cross_free = max(cross_free, now) + cross_us
+            crossed.append(cross_free + 1.0)
+            order.append((0, len(crossed) - 1))
+            continue
+        _, dims, _, size = units[first]
+        now = max(now, ready[first]) + 0.04 * size
+        level[first] += 1
+        order.append((level[first], first))
+        if level[first] in (1, 3):
+            dim, piece = (dims[0], piece_us * size) if level[first] == 1 else (dims[1], piece_us * size / 4)
+            ready[first] = max([send(dim, way, piece) for way in range(2)])
+            rest[first] = max([send(dim, way, piece) for way in range(2)])
+        elif level[first] in (2, 4):
+            dim, piece = (dims[0], piece_us * size) if level[first] == 2 else (dims[1], piece_us * size / 4)
+            ready[first] = max([rest[first]] + [send(dim, way, piece) for way in range(2)])
+        elif level[first] == 5:
+            piece = piece_us * size / 8
+            ready[first] = max([send(dims[2], way, piece) for way in range(2)])
+            ready[first] = max(ready[first], send(dims[2], first % 2, 2 * piece) + 0.7)
+    return order
+
+
+UNIT_LIST = make_units()
+UNITS = len(UNIT_LIST)
 
 
 def kernel(
@@ -51,8 +104,7 @@
     bucket_ref,
     hidden_ref,
     dout_ref,
-    sum_ref,
-    total_ref,
+    mean_ref,
     hidden_buf,
     lhs,
     dout_buf,
@@ -63,6 +115,7 @@
     third_in,
     tally,
     tally_in,
+    result,
     hidden_sem,
     dout_sem,
     cross_send,
@@ -77,6 +130,7 @@
     third_recv,
     tally_send,
     tally_recv,
+    result_sem,
 ):
     me = tuple(lax.axis_index(axis) for axis in AXES)
     core = me[3]
@@ -116,19 +170,15 @@
     for part in range(HIDDEN_CHUNKS):
         hidden_copy(part).wait()
 
-        def turn(step, carry, part=part):
-            row = pl.multiple_of(part * chunk + step * 128, 128)
-            position = lax.broadcasted_iota(jnp.int32, (128, WIDTH), 0) + row
-            live = jnp.where(position < own_count, 1.0, 0.0).astype(jnp.bfloat16)
-            masked = hidden_buf[pl.ds(row, 128), :] * live
-            lhs[:, pl.ds(row, 128)] = masked.T
-            return carry
-
-        lax.fori_loop(0, chunk // 128, turn, 0)
+        row = part * chunk
+        position = lax.broadcasted_iota(jnp.int32, (chunk, 128), 0) + row
+        live = jnp.where(position < own_count, 1.0, 0.0).astype(jnp.bfloat16)
+
+        for unit in range(0, WIDTH, 128):
+            masked = hidden_buf[pl.ds(row, chunk), pl.ds(unit, 128)] * live
+            lhs[pl.ds(unit, 128), pl.ds(row, chunk)] = masked.T
 
     tally[0] = jnp.full((8, 128), own_count, jnp.int32).astype(jnp.float32)
-
-    pl.semaphore_wait(barrier, 10)
 
     def remote(source, target, send, recv, device):
         return pltpu.make_async_remote_copy(
@@ -150,17 +200,13 @@
         slot = lax.rem(pair, THEIR_SLOTS)
         return remote(acc.at[slot], crossed.at[pair], cross_send.at[slot], cross_recv.at[pair], partner)
 
-    def product(pair, carry):
+    def product(pair):
         slot = lax.rem(pair, DOUT_SLOTS)
         dout_copy(pair).wait()
 
         @pl.when(pair + (DOUT_SLOTS - 1) < PAIRS)
         def _():
             dout_copy(pair + (DOUT_SLOTS - 1)).start()
-
-        @pl.when(pair >= THEIR_SLOTS)
-        def _():
-            left(acc.at[lax.rem(pair, THEIR_SLOTS)], cross_send.at[lax.rem(pair, THEIR_SLOTS)])
 
         theirs = lax.rem(pair, THEIR_SLOTS)
         mine = THEIR_SLOTS + pair
@@ -172,11 +218,6 @@
             value = value.reshape(2, 4, 4, 2, 8, PAIR)
             acc[place_0, 2 * half : 2 * half + 2] = value[:, :, :, 0]
             acc[place_1, 2 * half : 2 * half + 2] = value[:, :, :, 1]
-        cross_copy(pair).start()
-        return carry
-
-    def products(group):
-        lax.fori_loop(group[0][2], group[-1][2] + group[-1][3], product, 0)
 
     def at(where):
         return tuple(where.get(dim, slice(None)) for dim in range(3))
@@ -211,7 +252,7 @@
         copy = remote(
             acc.at[(pl.ds(THEIR_SLOTS + pair, size),) + region],
             first_in.at[pl.ds(pair, size), kind],
-            first_send.at[number],
+            first_send,
             recv.at[number],
             peer(order[0], (1, 3)[kind % 2]),
         )
@@ -226,7 +267,7 @@
         copy = remote(
             acc.at[(pl.ds(THEIR_SLOTS + pair, size),) + region],
             second_in.at[pl.ds(pair, size), kind],
-            second_send.at[number],
+            second_send,
             recv.at[number],
             peer(order[1], (1, 3)[kind % 2]),
         )
@@ -237,7 +278,7 @@
         return remote(
             acc.at[(pl.ds(THEIR_SLOTS + pair, size),) + third_region(order, shifted(order[2], by))],
             third_in.at[pl.ds(pair, size), by - 1],
-            third_send.at[number],
+            third_send,
             third_recv.at[number],
             peer(order[2], by),
         )
@@ -262,7 +303,6 @@
     def stage_3(unit):
         number, order, pair, size = unit
         arrived(first_in.at[pl.ds(pair, size), pl.ds(2, 4)], first_rest.at[number])
-        left(first_in.at[pl.ds(pair, size)], first_send.at[number])
         for side, (up, down) in enumerate(((4, 3), (2, 5))):
             region = first_region(order, me[order[0]], side)
             gather(pair, size, region, ((crossed, region), (first_in, (up,)), (first_in, (down,))))
@@ -280,23 +320,28 @@
     def stage_5(unit):
         number, order, pair, size = unit
         arrived(second_in.at[pl.ds(pair, size), pl.ds(2, 4)], second_rest.at[number])
-        left(second_in.at[pl.ds(pair, size)], second_send.at[number])
         for side, (up, down) in enumerate(((4, 3), (2, 5))):
             region = second_region(order, me[order[1]], side)
             gather(pair, size, region, ((second_in, (up,)), (second_in, (down,))))
         for by in (1, 2, 3):
             third_copy(unit, by).start()
 
+    def result_copy(unit):
+        number, order, pair, size = unit
+        columns = pl.ds(pair * PAIR, size * PAIR)
+        return pltpu.make_async_copy(result.at[:, columns], mean_ref.at[:, columns], result_sem)
+
     def stage_6(unit):
         number, order, pair, size = unit
         arrived(third_in.at[pl.ds(pair, size)], third_recv.at[number])
-        left(third_in.at[pl.ds(pair, size)], third_send.at[number])
         region = third_region(order, me[order[2]])
+        total = jnp.concatenate([tally[4]] * (PAIR // 128), axis=1)
         for step in range(size):
             value = acc[(THEIR_SLOTS + pair + step,) + region]
             for by in range(3):
                 value = value + third_in[pair + step, by]
-            sum_ref[:, pl.ds((pair + step) * PAIR, PAIR)] = value
+            result[:, pl.ds((pair + step) * PAIR, PAIR)] = value / total
+        result_copy(unit).start()
 
     def tally_start(level):
         if level == 0:
@@ -321,20 +366,50 @@
         tally[level + 1] = value
 
     stages = (stage_1, stage_2, stage_3, stage_4, stage_5, stage_6)
+    after = [[] for _ in range(PAIRS)]
+    done = -1
+    for level, number in list_schedule(UNIT_LIST):
+        if level == 0:
+            done = number
+        else:
+            after[done].append((level, number))
+
+    product(0)
+    pl.semaphore_wait(barrier, 10)
+    cross_copy(0).start()
     tally_start(0)
-    products(PLAN[0])
-    for step in range(len(PLAN) + len(stages) - 1):
-        if step + 1 < len(PLAN):
-            products(PLAN[step + 1])
-        for lag, stage in enumerate(stages):
-            if 0 <= step - lag < len(PLAN):
-                for unit in PLAN[step - lag]:
-                    stage(unit)
-        if step < 4:
-            tally_end(step)
-            if step < 3:
-                tally_start(step + 1)
-    total_ref[...] = tally[4]
+    for block in range(0, PAIRS, BLOCK):
+
+        def step(pair, carry, block=block):
+
+            @pl.when(pair >= THEIR_SLOTS)
+            def _():
+                left(acc.at[lax.rem(pair, THEIR_SLOTS)], cross_send.at[lax.rem(pair, THEIR_SLOTS)])
+
+            product(pair)
+            cross_copy(pair).start()
+            for offset in range(BLOCK):
+                last = block + offset
+                if last + 1 < PAIRS:
+
+                    @pl.when(pair == last)
+                    def _(last=last):
+                        for level, number in after[last]:
+                            stages[level - 1](UNIT_LIST[number])
+                        if last in TALLY_AFTER:
+                            tally_end(TALLY_AFTER.index(last))
+                            if last < TALLY_AFTER[-1]:
+                                tally_start(TALLY_AFTER.index(last) + 1)
+
+            return carry
+
+        lax.fori_loop(max(block, 1), block + BLOCK, step, 0)
+    for level, number in after[PAIRS - 1]:
+        stages[level - 1](UNIT_LIST[number])
+    left(first_in, first_send)
+    left(second_in, second_send)
+    left(third_in, third_send)
+    pltpu.make_async_copy(result, mean_ref, result_sem).wait()
     for slot in range(THEIR_SLOTS):
         left(acc.at[slot], cross_send.at[slot])
 
@@ -342,17 +417,13 @@
 def reduced(counts, bucket_expert, hidden, dout):
     f32 = jnp.float32
     dma = pltpu.SemaphoreType.DMA
-    vmem = pl.BlockSpec(memory_space=pltpu.VMEM)
     smem = pl.BlockSpec(memory_space=pltpu.SMEM)
     away = pl.BlockSpec(memory_space=pl.ANY)
     return pl.pallas_call(
         kernel,
-        out_shape=(
-            jax.ShapeDtypeStruct((8, PAIR * PAIRS), f32),
-            jax.ShapeDtypeStruct((8, 128), f32),
-        ),
+        out_shape=jax.ShapeDtypeStruct((8, PAIR * PAIRS), f32),
         in_specs=[smem, smem, away, away],
-        out_specs=(vmem, vmem),
+        out_specs=away,
         scratch_shapes=[
             pltpu.VMEM((ROWS, WIDTH), jnp.bfloat16),
             pltpu.VMEM((WIDTH, ROWS), jnp.bfloat16),
@@ -364,20 +435,22 @@
             pltpu.VMEM((PAIRS, 3, 8, PAIR), f32),
             pltpu.VMEM((5, 8, 128), f32),
             pltpu.VMEM((4, 3, 8, 128), f32),
+            pltpu.VMEM((8, PAIR * PAIRS), f32),
             dma((HIDDEN_CHUNKS,)),
             dma((DOUT_SLOTS,)),
             dma((THEIR_SLOTS,)),
             dma((PAIRS,)),
+            dma,
             dma((UNITS,)),
             dma((UNITS,)),
+            dma,
             dma((UNITS,)),
             dma((UNITS,)),
-            dma((UNITS,)),
-            dma((UNITS,)),
-            dma((UNITS,)),
+            dma,
             dma((UNITS,)),
             dma((4,)),
             dma((4,)),
+            dma,
         ],
         compiler_params=pltpu.CompilerParams(
             collective_id=0, has_side_effects=True, vmem_limit_bytes=67043328
@@ -386,8 +459,7 @@
 
 
 def body(hidden, dout, counts, bucket_expert, param, momentum):
-    summed, total = reduced(counts, bucket_expert, hidden, dout)
-    grad = summed / total[0, 0]
+    grad = reduced(counts, bucket_expert, hidden, dout)
     blend = first_beta * momentum + (1.0 - first_beta) * grad
     direction = jnp.tanh(blend / soft_width) + decay_rate * param
     new_param = param - learn_rate * direction

time: 92.3 us -> 79.4 us (0.86)
  Pallas kernels: 86.9 us -> 75.8 us
  local copies, waits for them, and re-layouts: 1.21 us -> 0 us
    pallas_call x1, Pallas kernels: 86.9 us -> 75.8 us  [reduced(): pl.pallas_call(kernel, out_shape=jax.ShapeDtypeStruct((8, PAIR * PAIRS),...]
    slice x1 -> x0, local copies, waits for them, and re-layouts: 1.21 us -> none  [body(): grad = summed / total[0, 0]]
where the time goes in v2:
time: 79.4 us; the launch traced here: 79.2 us
  Pallas kernels  75.8 us (95%)
  other arithmetic  2.08 us (3%)
  between operations  1.29 us (2%)
    pallas_call x1, Pallas kernels, reduced(): pl.pallas_call(kernel, out_shape=jax.ShapeDtypeStruct((8, PAIR * PAIRS),...  75.8 us
    sub x1, other arithmetic, body(): new_param = param - learn_rate * direction  2.08 us

profile of v2, /device:TPU:0, one launch (start us, length us, event | category | flops | bytes accessed | tf_op | source)
XLA Modules:
  0.0 79.2 jit_solution(919777165408939163)
XLA Ops:
  1.3 75.8 %shard_map.85 = f32[8,7168]{1,0:T(8,128)} custom-call(s32[1,256]{1,0:T(1,128)} %counts_ref.1, s32[1]{0:T(128)S(6)} %copy.9.bucket_ref, bf16[1536,1024]{1,0:T(8,128)(2,1)} %hidden_ref.1, bf16[1536,7168]{1,0:T(8,128)(2,1)} %dout_ref.1), custom_call_target="tpu_custom_call" | custom-call | tf_op jit(solution)/shard_map/pallas_call | solution.py:422
  77.1 2.1 %multiply_subtract_fusion = (f32[8,7168]{1,0:T(8,128)}, f32[8,7168]{1,0:T(8,128)}, f32[8,7168]{1,0:T(8,128)}) fusion(f32[8,7168]{1,0:T(8,128)} %param.10, f32[8,7168]{1,0:T(8,128)} %shard_map.85, f32[8,7168]{1,0:T(8,128)} %param.11), kind=kLoop, calls=%fused_computation.1 | loop fusion | flops 630784 | bytes 1376256 | tf_op jit(solution)/shard_map/sub | solution.py:465

commit v3 on v2

--- a/solution.py
+++ b/solution.py
@@ -23,80 +23,59 @@
 DOUT_SLOTS = 4
 HIDDEN_CHUNKS = 6
 
-SIZES = (
-    (1, 1, 1, 1, 1, 1, 1, 1, 1, 1),
-    (1, 1, 1, 1, 1, 1, 1, 1, 1),
-    (1, 1, 1, 1, 1, 1, 1, 1, 1),
+X, Y, Z = range(3)
+ORDERS = (
+    (X, Y, Z), (Y, X, Z), (Z, Y, X), (X, Z, Y),
+    (Y, Z, X), (Z, Y, X), (X, Y, Z), (Y, Z, X),
+    (Z, Y, X), (X, Y, Z), (Y, Z, X), (X, Z, Y),
+    (Z, Y, X), (X, Z, Y), (Z, X, Y), (Y, X, Z),
+    (Y, X, Z), (Z, Y, X), (Z, Y, X), (X, Z, Y),
+    (Y, X, Z), (X, Z, Y), (Y, X, Z), (X, Z, Y),
+    (Z, Y, X), (X, Z, Y), (Y, X, Z), (Z, Y, X),
 )
-ORDERS = ((0, 2, 1), (1, 0, 2), (2, 1, 0))
-SWAPPED = ((3, 6), (2, 4, 6), ())
-LEAD = 3
+DIRECT = (22, 25, 26)
+THIRD_ORDER = (
+    2, 7, 10, 22, 9, 3, 15, 4, 12, 5, 11, 18, 19, 8,
+    21, 26, 0, 16, 24, 14, 6, 1, 25, 27, 20, 13, 17, 23,
+)
+GROUP = 4
+EVENTS = (
+    (),
+    (),
+    (100,),
+    (101,),
+    (102,),
+    (103,),
+    (104,),
+    (105, 200),
+    (106, 201),
+    (107, 202),
+    (108, 203),
+    (109, 204),
+    (110, 205),
+    (111,),
+    (112, 206, 207, 302),
+    (113, 208),
+    (114,),
+    (115, 209),
+    (116, 210),
+    (117, 212),
+    (118, 211),
+    (119, 402),
+    (120,),
+    (121, 214, 215),
+    (122, 213),
+    (123, 216, 217),
+    (124,),
+    (125, 126, 219, 127, 220, 218, 221, 315, 222, 224, 223, 316, 314, 226, 227, 307, 301, 310, 303, 304, 311,
+        225, 309, 312, 305, 320, 318, 308, 319, 300, 322, 324, 502, 306, 321, 415, 313, 326, 327, 317, 409, 407,
+        412, 410, 323, 416, 403, 405, 414, 404, 418, 401, 408, 411, 400, 419, 424, 421, 325, 420, 406, 413, 427,
+        507, 510, 417, 423, 522, 509, 503, 515, 504, 512, 505, 511, 518, 519, 508, 521, 526, 500, 516, 524, 514,
+        506, 501, 525, 527, 520, 513, 517, 523, 600, 601, 602, 603, 604, 605, 606),
+)
 BLOCK = 4
 TALLY_AFTER = (3, 9, 15, 21)
-
-
-def make_units():
-    units = []
-    pair = 0
-    for turn in range(max(len(sizes) for sizes in SIZES)):
-        for colour, sizes in enumerate(SIZES):
-            if turn < len(sizes):
-                order = ORDERS[colour]
-                if turn in SWAPPED[colour]:
-                    order = (order[0], order[2], order[1])
-                units.append((len(units), order, pair, sizes[turn]))
-                pair += sizes[turn]
-    assert pair == PAIRS
-    return units
-
-
-def list_schedule(units):
-    product_us, cross_us, latency_us, piece_us = 1.03, 0.85, 2.0, 1.405
-    free = {(dim, way): 0.0 for dim in range(3) for way in range(2)}
-    level = [0] * len(units)
-    ready = [None] * len(units)
-    rest = [0.0] * len(units)
-    crossed = []
-    cross_free = 0.0
-    now = 0.0
-    order = []
-
-    def send(dim, way, duration):
-        free[dim, way] = max(free[dim, way], now) + duration
-        return free[dim, way] + latency_us
-
-    while min(level) < 6:
-        for number, (_, _, pair, size) in enumerate(units):
-            if level[number] == 0 and pair + size <= len(crossed):
-                ready[number] = max(crossed[pair : pair + size])
-        waiting = [n for n in range(len(units)) if level[n] < 6 and ready[n] is not None]
-        first = min(waiting, key=lambda n: (ready[n], n), default=None)
-        if len(crossed) < PAIRS and (len(crossed) < LEAD or first is None or ready[first] > now):
-            now += product_us
-            cross_free = max(cross_free, now) + cross_us
-            crossed.append(cross_free + 1.0)
-            order.append((0, len(crossed) - 1))
-            continue
-        _, dims, _, size = units[first]
-        now = max(now, ready[first]) + 0.04 * size
-        level[first] += 1
-        order.append((level[first], first))
-        if level[first] in (1, 3):
-            dim, piece = (dims[0], piece_us * size) if level[first] == 1 else (dims[1], piece_us * size / 4)
-            ready[first] = max([send(dim, way, piece) for way in range(2)])
-            rest[first] = max([send(dim, way, piece) for way in range(2)])
-        elif level[first] in (2, 4):
-            dim, piece = (dims[0], piece_us * size) if level[first] == 2 else (dims[1], piece_us * size / 4)
-            ready[first] = max([rest[first]] + [send(dim, way, piece) for way in range(2)])
-        elif level[first] == 5:
-            piece = piece_us * size / 8
-            ready[first] = max([send(dims[2], way, piece) for way in range(2)])
-            ready[first] = max(ready[first], send(dims[2], first % 2, 2 * piece) + 0.7)
-    return order
-
-
-UNIT_LIST = make_units()
-UNITS = len(UNIT_LIST)
+UNITS = len(ORDERS)
 
 
 def kernel(
@@ -273,13 +252,24 @@
         )
         return copy, region
 
+    def direct_copy(unit, by, side):
+        number, order, pair, size = unit
+        region = second_region(order, shifted(order[1], by), side)
+        return remote(
+            acc.at[(pl.ds(THEIR_SLOTS + pair, size),) + region],
+            second_in.at[pl.ds(pair, size), 2 * (by - 1) + side],
+            second_send,
+            second_rest.at[number],
+            peer(order[1], by),
+        )
+
     def third_copy(unit, by):
         number, order, pair, size = unit
         return remote(
             acc.at[(pl.ds(THEIR_SLOTS + pair, size),) + third_region(order, shifted(order[2], by))],
-            third_in.at[pl.ds(pair, size), by - 1],
+            third_in.at[pl.ds(THIRD_ORDER.index(number), size), by - 1],
             third_send,
-            third_recv.at[number],
+            third_recv.at[THIRD_ORDER.index(number) // GROUP],
             peer(order[2], by),
         )
 
@@ -306,8 +296,13 @@
         for side, (up, down) in enumerate(((4, 3), (2, 5))):
             region = first_region(order, me[order[0]], side)
             gather(pair, size, region, ((crossed, region), (first_in, (up,)), (first_in, (down,))))
-        for kind in range(4):
-            second_copy(unit, kind)[0].start()
+        if number in DIRECT:
+            for by in (1, 2, 3):
+                for side in range(2):
+                    direct_copy(unit, by, side).start()
+        else:
+            for kind in range(4):
+                second_copy(unit, kind)[0].start()
 
     def stage_4(unit):
         number, order, pair, size = unit
@@ -319,10 +314,16 @@
 
     def stage_5(unit):
         number, order, pair, size = unit
-        arrived(second_in.at[pl.ds(pair, size), pl.ds(2, 4)], second_rest.at[number])
+        if number in DIRECT:
+            arrived(second_in.at[pl.ds(pair, size)], second_rest.at[number])
+        else:
+            arrived(second_in.at[pl.ds(pair, size), pl.ds(2, 4)], second_rest.at[number])
         for side, (up, down) in enumerate(((4, 3), (2, 5))):
             region = second_region(order, me[order[1]], side)
-            gather(pair, size, region, ((second_in, (up,)), (second_in, (down,))))
+            if number in DIRECT:
+                gather(pair, size, region, tuple((second_in, (2 * by + side,)) for by in range(3)))
+            else:
+                gather(pair, size, region, ((second_in, (up,)), (second_in, (down,))))
         for by in (1, 2, 3):
             third_copy(unit, by).start()
 
@@ -331,17 +332,17 @@
         columns = pl.ds(pair * PAIR, size * PAIR)
         return pltpu.make_async_copy(result.at[:, columns], mean_ref.at[:, columns], result_sem)
 
-    def stage_6(unit):
-        number, order, pair, size = unit
-        arrived(third_in.at[pl.ds(pair, size)], third_recv.at[number])
-        region = third_region(order, me[order[2]])
+    def stage_6(group):
+        arrived(third_in.at[pl.ds(group * GROUP, GROUP)], third_recv.at[group])
         total = jnp.concatenate([tally[4]] * (PAIR // 128), axis=1)
-        for step in range(size):
-            value = acc[(THEIR_SLOTS + pair + step,) + region]
+        for rank in range(group * GROUP, (group + 1) * GROUP):
+            unit = unit_of(THIRD_ORDER[rank])
+            number, order, pair, size = unit
+            value = acc[(THEIR_SLOTS + pair,) + third_region(order, me[order[2]])]
             for by in range(3):
-                value = value + third_in[pair + step, by]
-            result[:, pl.ds((pair + step) * PAIR, PAIR)] = value / total
-        result_copy(unit).start()
+                value = value + third_in[rank, by]
+            result[:, pl.ds(pair * PAIR, PAIR)] = value / total
+            result_copy(unit).start()
 
     def tally_start(level):
         if level == 0:
@@ -365,14 +366,18 @@
             value = value + tally_in[level, by]
         tally[level + 1] = value
 
-    stages = (stage_1, stage_2, stage_3, stage_4, stage_5, stage_6)
-    after = [[] for _ in range(PAIRS)]
-    done = -1
-    for level, number in list_schedule(UNIT_LIST):
-        if level == 0:
-            done = number
-        else:
-            after[done].append((level, number))
+    def unit_of(number):
+        return number, ORDERS[number], number, 1
+
+    stages = (stage_1, stage_2, stage_3, stage_4, stage_5)
+
+    def events(last):
+        for event in EVENTS[last]:
+            level, number = divmod(event, 100)
+            if level == 6:
+                stage_6(number)
+            else:
+                stages[level - 1](unit_of(number))
 
     product(0)
     pl.semaphore_wait(barrier, 10)
@@ -394,8 +399,7 @@
 
                     @pl.when(pair == last)
                     def _(last=last):
-                        for level, number in after[last]:
-                            stages[level - 1](UNIT_LIST[number])
+                        events(last)
                         if last in TALLY_AFTER:
                             tally_end(TALLY_AFTER.index(last))
                             if last < TALLY_AFTER[-1]:
@@ -404,8 +408,7 @@
             return carry
 
         lax.fori_loop(max(block, 1), block + BLOCK, step, 0)
-    for level, number in after[PAIRS - 1]:
-        stages[level - 1](UNIT_LIST[number])
+    events(PAIRS - 1)
     left(first_in, first_send)
     left(second_in, second_send)
     left(third_in, third_send)
@@ -447,7 +450,7 @@
             dma((UNITS,)),
             dma((UNITS,)),
             dma,
-            dma((UNITS,)),
+            dma((UNITS // GROUP,)),
             dma((4,)),
             dma((4,)),
             dma,

time: 79.4 us -> 74.7 us (0.941)
  Pallas kernels: 75.8 us -> 70.7 us
    pallas_call x1, Pallas kernels: 75.8 us -> 70.7 us  [reduced(): pl.pallas_call(kernel, out_shape=jax.ShapeDtypeStruct((8, PAIR * PAIRS),...]
where the time goes in v3:
time: 74.7 us; the launch traced here: 74.1 us
  Pallas kernels  70.7 us (95%)
  other arithmetic  2.08 us (3%)
  between operations  1.29 us (2%)
    pallas_call x1, Pallas kernels, reduced(): pl.pallas_call(kernel, out_shape=jax.ShapeDtypeStruct((8, PAIR * PAIRS),...  70.7 us
    sub x1, other arithmetic, body(): new_param = param - learn_rate * direction  2.08 us

profile of v3, /device:TPU:0, one launch (start us, length us, event | category | flops | bytes accessed | tf_op | source)
XLA Modules:
  0.0 74.1 jit_solution(446834828327477442)
XLA Ops:
  1.3 70.7 %shard_map.85 = f32[8,7168]{1,0:T(8,128)} custom-call(s32[1,256]{1,0:T(1,128)} %counts_ref.1, s32[1]{0:T(128)S(6)} %copy.9.bucket_ref, bf16[1536,1024]{1,0:T(8,128)(2,1)} %hidden_ref.1, bf16[1536,7168]{1,0:T(8,128)(2,1)} %dout_ref.1), custom_call_target="tpu_custom_call" | custom-call | tf_op jit(solution)/shard_map/pallas_call | solution.py:425
  72.0 2.1 %multiply_subtract_fusion = (f32[8,7168]{1,0:T(8,128)}, f32[8,7168]{1,0:T(8,128)}, f32[8,7168]{1,0:T(8,128)}) fusion(f32[8,7168]{1,0:T(8,128)} %param.10, f32[8,7168]{1,0:T(8,128)} %shard_map.85, f32[8,7168]{1,0:T(8,128)} %param.11), kind=kLoop, calls=%fused_computation.1 | loop fusion | flops 630784 | bytes 1376256 | tf_op jit(solution)/shard_map/sub | solution.py:468

commit v4 on v3

--- a/solution.py
+++ b/solution.py
@@ -25,18 +25,18 @@
 
 X, Y, Z = range(3)
 ORDERS = (
-    (X, Y, Z), (Y, X, Z), (Z, Y, X), (X, Z, Y),
-    (Y, Z, X), (Z, Y, X), (X, Y, Z), (Y, Z, X),
-    (Z, Y, X), (X, Y, Z), (Y, Z, X), (X, Z, Y),
-    (Z, Y, X), (X, Z, Y), (Z, X, Y), (Y, X, Z),
-    (Y, X, Z), (Z, Y, X), (Z, Y, X), (X, Z, Y),
-    (Y, X, Z), (X, Z, Y), (Y, X, Z), (X, Z, Y),
-    (Z, Y, X), (X, Z, Y), (Y, X, Z), (Z, Y, X),
+    (X, Y, Z), (Y, X, Z), (Z, X, Y), (X, Z, Y),
+    (Y, X, Z), (Z, X, Y), (X, Z, Y), (Y, X, Z),
+    (Z, Y, X), (X, Y, Z), (X, Y, Z), (Y, X, Z),
+    (Z, Y, X), (Y, Z, X), (Z, Y, X), (Y, Z, X),
+    (Y, X, Z), (X, Z, Y), (Y, X, Z), (Z, Y, X),
+    (X, Z, Y), (Y, Z, X), (X, Z, Y), (Z, Y, X),
+    (X, Z, Y), (Z, Y, X), (Z, Y, X), (X, Y, Z),
 )
-DIRECT = (22, 25, 26)
+DIRECT = (7, 24, 27)
 THIRD_ORDER = (
-    2, 7, 10, 22, 9, 3, 15, 4, 12, 5, 11, 18, 19, 8,
-    21, 26, 0, 16, 24, 14, 6, 1, 25, 27, 20, 13, 17, 23,
+    9, 13, 4, 17, 0, 19, 12, 1, 14, 24, 8, 15, 3, 7,
+    20, 27, 6, 16, 23, 22, 2, 25, 21, 18, 10, 5, 26, 11,
 )
 GROUP = 4
 EVENTS = (
@@ -52,26 +52,26 @@
     (107, 202),
     (108, 203),
     (109, 204),
-    (110, 205),
+    (110, 205, 300),
     (111,),
-    (112, 206, 207, 302),
-    (113, 208),
-    (114,),
-    (115, 209),
-    (116, 210),
-    (117, 212),
-    (118, 211),
-    (119, 402),
-    (120,),
-    (121, 214, 215),
-    (122, 213),
-    (123, 216, 217),
-    (124,),
-    (125, 126, 219, 127, 220, 218, 221, 315, 222, 224, 223, 316, 314, 226, 227, 307, 301, 310, 303, 304, 311,
-        225, 309, 312, 305, 320, 318, 308, 319, 300, 322, 324, 502, 306, 321, 415, 313, 326, 327, 317, 409, 407,
-        412, 410, 323, 416, 403, 405, 414, 404, 418, 401, 408, 411, 400, 419, 424, 421, 325, 420, 406, 413, 427,
-        507, 510, 417, 423, 522, 509, 503, 515, 504, 512, 505, 511, 518, 519, 508, 521, 526, 500, 516, 524, 514,
-        506, 501, 525, 527, 520, 513, 517, 523, 600, 601, 602, 603, 604, 605, 606),
+    (112, 206),
+    (113, 207),
+    (114, 208),
+    (115, 209, 304, 400),
+    (116,),
+    (117, 211, 212),
+    (118, 210),
+    (119,),
+    (120, 213, 214),
+    (121,),
+    (122, 309, 404),
+    (123, 215),
+    (124, 217),
+    (125, 219, 126, 216, 127, 220, 223, 222, 218, 225, 313, 224, 301, 221, 319, 312, 226, 314, 317, 409, 227,
+        315, 308, 303, 323, 316, 302, 325, 320, 413, 318, 306, 322, 305, 310, 321, 326, 311, 419, 417, 324, 412,
+        415, 401, 414, 403, 307, 509, 420, 408, 327, 513, 416, 423, 406, 402, 425, 422, 418, 410, 421, 504, 405,
+        426, 517, 500, 411, 519, 512, 501, 514, 524, 508, 515, 503, 507, 520, 527, 506, 516, 523, 522, 502, 525,
+        521, 518, 510, 505, 526, 511, 600, 601, 602, 603, 604, 605, 606),
 )
 BLOCK = 4
 TALLY_AFTER = (3, 9, 15, 21)
@@ -79,8 +79,8 @@
 
 
 def kernel(
-    counts_ref,
-    bucket_ref,
+    counts_hbm,
+    bucket_hbm,
     hidden_ref,
     dout_ref,
     mean_ref,
@@ -95,6 +95,9 @@
     tally,
     tally_in,
     result,
+    counts_ref,
+    bucket_ref,
+    scalar_sem,
     hidden_sem,
     dout_sem,
     cross_send,
@@ -122,28 +125,38 @@
 
     partner = (me[0], me[1], me[2], 1 - core)
 
+    chunk = ROWS // HIDDEN_CHUNKS
+
+    def hidden_copy(part):
+        rows = pl.ds(part * chunk, chunk)
+        return pltpu.make_async_copy(hidden_ref.at[rows], hidden_buf.at[rows], hidden_sem.at[part])
+
+    def dout_copy(pair):
+        slot = lax.rem(pair, DOUT_SLOTS)
+        columns = pl.ds(pl.multiple_of(pair * PAIR, PAIR), PAIR)
+        return pltpu.make_async_copy(dout_ref.at[:, columns], dout_buf.at[slot], dout_sem.at[slot])
+
+    scalars = (
+        pltpu.make_async_copy(counts_hbm, counts_ref, scalar_sem.at[0]),
+        pltpu.make_async_copy(bucket_hbm, bucket_ref, scalar_sem.at[1]),
+    )
+    for copy in scalars:
+        copy.start()
+    hidden_copy(0).start()
+
     barrier = pltpu.get_barrier_semaphore()
     pl.semaphore_signal(barrier, inc=1, device_id=partner, device_id_type=MESH)
     for dim in range(3):
         for by in (1, 2, 3):
             pl.semaphore_signal(barrier, inc=1, device_id=peer(dim, by), device_id_type=MESH)
 
-    chunk = ROWS // HIDDEN_CHUNKS
-
-    def hidden_copy(part):
-        rows = pl.ds(part * chunk, chunk)
-        return pltpu.make_async_copy(hidden_ref.at[rows], hidden_buf.at[rows], hidden_sem.at[part])
-
-    def dout_copy(pair):
-        slot = lax.rem(pair, DOUT_SLOTS)
-        columns = pl.ds(pl.multiple_of(pair * PAIR, PAIR), PAIR)
-        return pltpu.make_async_copy(dout_ref.at[:, columns], dout_buf.at[slot], dout_sem.at[slot])
-
-    for part in range(HIDDEN_CHUNKS):
+    for part in range(1, HIDDEN_CHUNKS):
         hidden_copy(part).start()
     for pair in range(DOUT_SLOTS - 1):
         dout_copy(pair).start()
 
+    for copy in scalars:
+        copy.wait()
     own_count = counts_ref[0, bucket_ref[0]]
 
     for part in range(HIDDEN_CHUNKS):
@@ -420,12 +433,11 @@
 def reduced(counts, bucket_expert, hidden, dout):
     f32 = jnp.float32
     dma = pltpu.SemaphoreType.DMA
-    smem = pl.BlockSpec(memory_space=pltpu.SMEM)
     away = pl.BlockSpec(memory_space=pl.ANY)
     return pl.pallas_call(
         kernel,
         out_shape=jax.ShapeDtypeStruct((8, PAIR * PAIRS), f32),
-        in_specs=[smem, smem, away, away],
+        in_specs=[away] * 4,
         out_specs=away,
         scratch_shapes=[
             pltpu.VMEM((ROWS, WIDTH), jnp.bfloat16),
@@ -439,6 +451,9 @@
             pltpu.VMEM((5, 8, 128), f32),
             pltpu.VMEM((4, 3, 8, 128), f32),
             pltpu.VMEM((8, PAIR * PAIRS), f32),
+            pltpu.SMEM((1, 256), jnp.int32),
+            pltpu.SMEM((1,), jnp.int32),
+            dma((2,)),
             dma((HIDDEN_CHUNKS,)),
             dma((DOUT_SLOTS,)),
             dma((THEIR_SLOTS,)),

time: 74.7 us -> 73.3 us (0.981)
  Pallas kernels: 70.7 us -> 69.8 us
    pallas_call x1, Pallas kernels: 70.7 us -> 69.8 us  [reduced(): pl.pallas_call(kernel, out_shape=jax.ShapeDtypeStruct((8, PAIR * PAIRS),...]
where the time goes in v4:
time: 73.3 us; the launch traced here: 73.2 us
  Pallas kernels  69.8 us (95%)
  other arithmetic  2.08 us (3%)
  between operations  1.29 us (2%)
    pallas_call x1, Pallas kernels, reduced(): pl.pallas_call(kernel, out_shape=jax.ShapeDtypeStruct((8, PAIR * PAIRS),...  69.8 us
    sub x1, other arithmetic, body(): new_param = param - learn_rate * direction  2.08 us

profile of v4, /device:TPU:0, one launch (start us, length us, event | category | flops | bytes accessed | tf_op | source)
XLA Modules:
  0.0 73.2 jit_solution(9018586327060175098)
XLA Ops:
  1.3 69.8 %shard_map.85 = f32[8,7168]{1,0:T(8,128)} custom-call(s32[1,256]{1,0:T(1,128)} %counts_hbm.1, s32[1]{0:T(128)S(6)} %copy.9.bucket_hbm, bf16[1536,1024]{1,0:T(8,128)(2,1)} %hidden_ref.1, bf16[1536,7168]{1,0:T(8,128)(2,1)} %dout_ref.1), custom_call_target="tpu_custom_call" | custom-call | tf_op jit(solution)/shard_map/pallas_call | solution.py:437
  71.1 2.1 %multiply_subtract_fusion = (f32[8,7168]{1,0:T(8,128)}, f32[8,7168]{1,0:T(8,128)}, f32[8,7168]{1,0:T(8,128)}) fusion(f32[8,7168]{1,0:T(8,128)} %param.10, f32[8,7168]{1,0:T(8,128)} %shard_map.85, f32[8,7168]{1,0:T(8,128)} %param.11), kind=kLoop, calls=%fused_computation.1 | loop fusion | flops 630784 | bytes 1376256 | tf_op jit(solution)/shard_map/sub | solution.py:483

commit v5 on v4

--- a/solution.py
+++ b/solution.py
@@ -113,6 +113,7 @@
     tally_send,
     tally_recv,
     result_sem,
+    far,
 ):
     me = tuple(lax.axis_index(axis) for axis in AXES)
     core = me[3]
@@ -147,7 +148,7 @@
     barrier = pltpu.get_barrier_semaphore()
     pl.semaphore_signal(barrier, inc=1, device_id=partner, device_id_type=MESH)
     for dim in range(3):
-        for by in (1, 2, 3):
+        for by in (1, 3):
             pl.semaphore_signal(barrier, inc=1, device_id=peer(dim, by), device_id_type=MESH)
 
     for part in range(1, HIDDEN_CHUNKS):
@@ -393,7 +394,9 @@
                 stages[level - 1](unit_of(number))
 
     product(0)
-    pl.semaphore_wait(barrier, 10)
+    pl.semaphore_wait(barrier, 7)
+    for dim in range(3):
+        pl.semaphore_signal(far, inc=1, device_id=peer(dim, 3), device_id_type=MESH)
     cross_copy(0).start()
     tally_start(0)
     for block in range(0, PAIRS, BLOCK):
@@ -413,6 +416,8 @@
                     @pl.when(pair == last)
                     def _(last=last):
                         events(last)
+                        if last == TALLY_AFTER[0]:
+                            pl.semaphore_wait(far, 3)
                         if last in TALLY_AFTER:
                             tally_end(TALLY_AFTER.index(last))
                             if last < TALLY_AFTER[-1]:
@@ -469,6 +474,7 @@
             dma((4,)),
             dma((4,)),
             dma,
+            pltpu.SemaphoreType.REGULAR,
         ],
         compiler_params=pltpu.CompilerParams(
             collective_id=0, has_side_effects=True, vmem_limit_bytes=67043328

time: 73.3 us -> 73.3 us (level)
  no operation moved by 1% of the time
where the time goes in v5:
time: 73.3 us; the launch traced here: 73.2 us
  Pallas kernels  69.8 us (95%)
  other arithmetic  2.08 us (3%)
  between operations  1.29 us (2%)
    pallas_call x1, Pallas kernels, reduced(): pl.pallas_call(kernel, out_shape=jax.ShapeDtypeStruct((8, PAIR * PAIRS),...  69.8 us
    sub x1, other arithmetic, body(): new_param = param - learn_rate * direction  2.08 us

profile of v5, /device:TPU:0, one launch (start us, length us, event | category | flops | bytes accessed | tf_op | source)
XLA Modules:
  0.0 73.2 jit_solution(7031880747535438459)
XLA Ops:
  1.3 69.8 %shard_map.85 = f32[8,7168]{1,0:T(8,128)} custom-call(s32[1,256]{1,0:T(1,128)} %counts_hbm.1, s32[1]{0:T(128)S(6)} %copy.9.bucket_hbm, bf16[1536,1024]{1,0:T(8,128)(2,1)} %hidden_ref.1, bf16[1536,7168]{1,0:T(8,128)(2,1)} %dout_ref.1), custom_call_target="tpu_custom_call" | custom-call | tf_op jit(solution)/shard_map/pallas_call | solution.py:442
  71.1 2.1 %multiply_subtract_fusion = (f32[8,7168]{1,0:T(8,128)}, f32[8,7168]{1,0:T(8,128)}, f32[8,7168]{1,0:T(8,128)}) fusion(f32[8,7168]{1,0:T(8,128)} %param.10, f32[8,7168]{1,0:T(8,128)} %shard_map.85, f32[8,7168]{1,0:T(8,128)} %param.11), kind=kLoop, calls=%fused_computation.1 | loop fusion | flops 630784 | bytes 1376256 | tf_op jit(solution)/shard_map/sub | solution.py:489
